TPU v7x, 32 devices: a whole 2x2x4 slice. The times are simulated.
32 devices in a mesh: fsdp: 8 (over z, y), tp: 4 (over x, core).
Axes of the slice: x: 2, y: 2, z: 4, core: 2. Of those that a mesh axis runs over, the one named last changes fastest.
Arguments:
- x: bfloat16 [32768, 4096], P(('fsdp', 'tp'))
- gamma: float32 [4096], replicated
- w1: bfloat16 [4096, 14336], P('fsdp', 'tp')
- w2: bfloat16 [14336, 4096], P('tp', 'fsdp')
Outputs:
- output: bfloat16 [32768, 4096], P(('fsdp', 'tp'))
All inputs are finite; a program needn't handle non-finite values.
Results may differ from a plain program's by a relative error of at most 0.001.
Values are sent between devices in bfloat16 or wider.
A program may use at most 1 GiB of HBM per device.

v0:
```python
import jax
import jax.numpy as jnp
from jax import lax
from jax.sharding import PartitionSpec as P

EPS = 1e-6


def _norm(x, gamma):
    xf = x.astype(jnp.float32)
    mu = jnp.mean(xf, axis=-1, keepdims=True)
    var = jnp.mean(jnp.square(xf - mu), axis=-1, keepdims=True)
    return xf, ((xf - mu) * lax.rsqrt(var + EPS) * gamma).astype(jnp.bfloat16)


def solution(mesh):
    def body(x, gamma, w1, w2):
        w1f = lax.all_gather(w1, "fsdp", axis=0, tiled=True)
        w2f = lax.all_gather(w2, "fsdp", axis=1, tiled=True)
        xf, xn = _norm(x, gamma)
        xg = lax.all_gather(xn, "tp", axis=0, tiled=True)
        h = jax.nn.gelu(jnp.dot(xg, w1f, preferred_element_type=jnp.float32), approximate=True).astype(jnp.bfloat16)
        yp = jnp.dot(h, w2f, preferred_element_type=jnp.float32)
        y = lax.psum_scatter(yp, "tp", scatter_dimension=0, tiled=True)
        return (xf + y).astype(jnp.bfloat16)

    return jax.shard_map(
        body,
        mesh=mesh,
        in_specs=(P(("fsdp", "tp"), None), P(None), P("fsdp", "tp"), P("tp", "fsdp")),
        out_specs=P(("fsdp", "tp"), None),
        check_vma=False,
    )
```

profile of v0, /device:TPU:0, one launch (start us, length us, event | category | flops | bytes accessed | tf_op | source)
XLA Modules:
  0.0 1954.7 jit_solution(3209983819520671780)
XLA Ops:
  6.5 0.0 all-gather.4.cloned.1.call-start
  6.5 4.5 convert_reduce_fusion
  11.1 5.7 fusion.16
  16.8 11.4 fusion.18
  28.2 0.0 all-gather.4.cloned.1.call-update
  28.2 0.0 all-gather.6.cloned.1.call-start
  28.2 0.7 all-gather.6.cloned.1.call-update
  28.9 0.0 all-gather.8.cloned.1.call-start
  29.0 0.7 all-gather.8.cloned.1.call-update
  29.7 0.2 reduce-scatter.4.cloned.1.call-start
  29.9 203.3 %all-gather.4.cloned.1.call-done = bf16[4096,4096]{1,0:T(8,128)(2,1)} async-done(((bf16[1024,4096]{1,0:T(8,128)(2,1)}), bf16[4096,4096]{1,0:T(8,128)(2,1)}) %all-gather.4.cloned.1.call-update) | async-done | bytes 33554448 | tf_op jit(solution)/shard_map/all_gather | solution.py:21
  233.2 553.4 %all-gather.6.cloned.1.call-done = bf16[4096,3584]{1,0:T(8,128)(2,1)} async-done(((bf16[512,3584]{1,0:T(8,128)(2,1)}), bf16[4096,3584]{1,0:T(8,128)(2,1)}) %all-gather.6.cloned.1.call-update) | async-done | bytes 29360144 | tf_op jit(solution)/shard_map/all_gather | solution.py:18
  786.6 134.0 %fusion.24 = f32[4096,3584]{1,0:T(8,128)} fusion(bf16[4096,4096]{1,0:T(8,128)(2,1)} %all-gather.4.cloned.1.call-done, bf16[4096,3584]{1,0:T(8,128)(2,1)} %all-gather.6.cloned.1.call-done), kind=kOutput, calls=%fused_computation.29 | convolution fusion | flops 120259084288 | bytes 121634816 | tf_op jit(solution)/shard_map/dot_general | solution.py:22
  920.6 422.7 %all-gather.8.cloned.1.call-done = bf16[3584,4096]{1,0:T(8,128)(2,1)} async-done(((bf16[3584,512]{1,0:T(8,128)(2,1)}), bf16[3584,4096]{1,0:T(8,128)(2,1)}) %all-gather.8.cloned.1.call-update) | async-done | bytes 29360144 | tf_op jit(solution)/shard_map/all_gather | solution.py:19
  1343.3 143.2 %fusion.8 = f32[4096,4096]{1,0:T(8,128)} fusion(bf16[3584,4096]{1,0:T(8,128)(2,1)} %all-gather.8.cloned.1.call-done, f32[4096,3584]{1,0:T(8,128)} %fusion.24), kind=kOutput, calls=%fused_computation.9 | convolution fusion | flops 120391204864 | bytes 155189248 | tf_op jit(solution)/shard_map/dot_general | solution.py:23
  1486.6 0.0 reduce-scatter.4.cloned.1.call-update
  1486.6 449.6 %reduce-scatter.4.cloned.1.call-done = f32[1024,4096]{1,0:T(8,128)} async-done(((f32[4096,4096]{1,0:T(8,128)}), f32[1024,4096]{1,0:T(8,128)}) %reduce-scatter.4.cloned.1.call-update) | async-done | bytes 16777232
  1936.2 12.0 fusion.19
  (2 shorter events, 0.0 us)
Async XLA Ops:
  6.5 226.7 %all-gather.4.cloned.1.call-start = ((), (), s32[]{:S(2)}) async-start(), calls=%async_computation.1 | async-start | bytes 41943040 | tf_op jit(solution)/shard_map/all_gather | solution.py:21
  28.2 758.4 %all-gather.6.cloned.1.call-start = ((), (), s32[]{:S(2)}) async-start(), calls=%async_computation.2 | async-start | bytes 33030144 | tf_op jit(solution)/shard_map/all_gather | solution.py:18
  28.9 1314.4 %all-gather.8.cloned.1.call-start = ((), (), s32[]{:S(2)}) async-start(), calls=%async_computation.3 | async-start | bytes 33030144 | tf_op jit(solution)/shard_map/all_gather | solution.py:19
  29.7 1906.5 %reduce-scatter.4.cloned.1.call-start = ((), (), s32[]{:S(2)}) async-start(), calls=%async_computation.4 | async-start | bytes 83886080
Sparse Core Ops, SparseCore 0:
  28.3 204.8 all-gather.3
  234.8 551.8 all-gather.5
  788.1 555.1 all-gather.7
  1486.7 449.4 reduce-scatter.3
where the time goes:
time: 1950 us
  waiting for transfers between devices  1630 us (84%)
  matrix products  277 us (14%)
  other arithmetic  33.6 us (2%)
    all_gather x1, waiting for transfers between devices, body(): w1f = lax.all_gather(w1, 'fsdp', axis=0, tiled=True)  553 us
    unnamed x5, waiting for transfers between devices  451 us
    all_gather x1, waiting for transfers between devices, body(): w2f = lax.all_gather(w2, 'fsdp', axis=1, tiled=True)  423 us
    all_gather x1, waiting for transfers between devices, body(): xg = lax.all_gather(xn, 'tp', axis=0, tiled=True)  203 us
    dot_general x1, matrix products, body(): yp = jnp.dot(h, w2f, preferred_element_type=jnp.float32)  143 us
    dot_general x1, matrix products, body(): jnp.dot(xg, w1f, preferred_element_type=jnp.float32)  134 us
  transfers between devices with their start and end apart: 4, of which 4 were waited for; matrix products, arithmetic and copies ran while one was open for 7% of the time, Pallas kernels for 0%

commit v1 on v0

v1 whole, which is shorter than its diff:
```python
import functools

import jax
import jax.numpy as jnp
from jax import lax
from jax.experimental import pallas as pl
from jax.experimental.pallas import tpu as pltpu
from jax.sharding import PartitionSpec as P

EPS = 1e-6
MESH = pl.DeviceIdType.MESH
BF16, F32 = jnp.bfloat16, jnp.float32

D = 4096
FS = 3584
ROWS = 1024
NC = 7
CW = FS // NC
KB = D // 8
PR = 512
HR = PR // 2


def _kernel(
    x_ref, gamma_ref, w1_ref, w2_ref,
    y_ref, xg, hg, w2g, d2d, sbuf, rs, sibp,
    w1v, xbuf, hbuf, wbuf, ubuf, dbuf, stage, tbuf, sibv, rsv, xtv, obuf,
    w1_send, w1_recv, w2_send, w2_recv, x_send, x_recv,
    dd_send, dd_recv, rs_send, rs_recv, sp_send, sp_recv,
    l_sem, loc_sem,
):
    a, b = lax.axis_index("fsdp"), lax.axis_index("tp")
    z, yq = a // 2, a % 2
    c = b % 2
    zp, zm, z2 = ((z + 1) % 4) * 2 + yq, ((z + 3) % 4) * 2 + yq, ((z + 2) % 4) * 2 + yq
    yy = z * 2 + (1 - yq)
    zpy, zmy, z2y = ((z + 1) % 4) * 2 + 1 - yq, ((z + 3) % 4) * 2 + 1 - yq, ((z + 2) % 4) * 2 + 1 - yq
    to_zp, to_zm, to_yy = (zp, b), (zm, b), (yy, b)
    sib = (a, (b // 2) * 2 + 1 - c)
    par = (a, (1 - b // 2) * 2 + c)

    barrier = pltpu.get_barrier_semaphore()
    for dev in (to_zp, to_zm, to_yy, sib, par):
        pl.semaphore_signal(barrier, inc=1, device_id=dev, device_id_type=MESH)
    pl.semaphore_wait(barrier, 5)

    def remote(src, dst, ssem, rsem, dev):
        return pltpu.make_async_remote_copy(
            src_ref=src, dst_ref=dst, send_sem=ssem, recv_sem=rsem, device_id=dev, device_id_type=MESH
        )

    sends = {}

    def w1_reg(j, s, lo, n):
        return w1v.at[j, pl.ds(pl.multiple_of(s * KB + lo, HR), n), :]

    def w1_msg(j, m, dev, s, lo=0, n=KB, own=False):
        dst = w1_reg(j, s, lo, n)
        src = w1_ref.at[:, pl.ds(j * CW, CW)] if own else dst
        cp = remote(src, dst, w1_send.at[j, m], w1_recv.at[j, m], dev)
        cp.start()
        sends[(j, m)] = cp

    def w1_got(j, m):
        sends[(j, m)].wait_recv()

    loc = {}

    def s0(j):
        w1_msg(j, 0, to_yy, a, own=True)
        w1_msg(j, 1, to_zp, a, own=True)
        w1_msg(j, 2, to_zm, a, own=True)
        cp = pltpu.make_async_copy(w1_ref.at[:, pl.ds(j * CW, CW)], w1_reg(j, a, 0, KB), loc_sem.at[j])
        cp.start()
        loc[j] = cp

    def s1(j):
        w1_got(j, 0)
        if j % 2 == 0:
            w1_msg(j, 3, to_zp, yy)
            w1_msg(j, 4, to_zm, yy)
        w1_got(j, 1)
        w1_got(j, 2)
        w1_msg(j, 5, to_zp, zm, 0, HR)
        w1_msg(j, 6, to_zm, zp, HR, HR)
        if j % 2 == 1:
            w1_msg(j, 3, to_yy, zm)
            w1_msg(j, 4, to_yy, zp)

    def s2(j):
        if j % 2 == 0:
            w1_got(j, 3)
            w1_msg(j, 7, to_zp, zmy, 0, HR)
            w1_got(j, 4)
            w1_msg(j, 8, to_zm, zpy, HR, HR)
            w1_got(j, 5)
            w1_got(j, 6)
        else:
            w1_got(j, 5)
            w1_got(j, 6)
            w1_msg(j, 7, to_yy, z2)
            w1_got(j, 3)
            w1_got(j, 4)

    def s3(j):
        w1_got(j, 7)
        if j % 2 == 0:
            w1_got(j, 8)
        loc[j].wait()

    def w2_msg(m, dev, s, lo=0, n=FS, own=False):
        dst = w2g.at[s, pl.ds(lo, n), :]
        src = w2_ref if own else dst
        return remote(src, dst, w2_send.at[m], w2_recv.at[m], dev)

    H2 = FS // 2
    w2m = [
        w2_msg(0, to_yy, a, own=True),
        w2_msg(1, to_zp, a, own=True),
        w2_msg(2, to_zm, a, own=True),
        w2_msg(3, to_zp, zm, 0, H2),
        w2_msg(4, to_zm, zp, H2, H2),
        w2_msg(5, to_yy, zm),
        w2_msg(6, to_yy, zp),
        w2_msg(7, to_yy, z2),
    ]

    s0(0)
    s0(1)
    s0(2)

    def x_in(r):
        return pltpu.make_async_copy(x_ref.at[pl.ds(r * HR, HR), :], xbuf.at[r % 2, pl.ds(0, HR), :], l_sem.at[r % 2])

    xs = {}
    x_in(0).start()
    for r in range(4):
        if r < 3:
            x_in(r + 1).start()
        x_in(r).wait()
        s = r % 2

        @pl.loop(0, HR // 32)
        def _(g):
            xf = xbuf[s, pl.ds(g * 32, 32), :].astype(F32)
            mu = jnp.mean(xf, axis=-1, keepdims=True)
            xc = xf - mu
            var = jnp.mean(jnp.square(xc), axis=-1, keepdims=True)
            xbuf[s, pl.ds(HR + g * 32, 32), :] = (xc * lax.rsqrt(var + EPS) * gamma_ref[...]).astype(BF16)

        mine = xg.at[pl.ds(r * HR, HR), :]
        cp = pltpu.make_async_copy(xbuf.at[s, pl.ds(HR, HR), :], mine, l_sem.at[2])
        cp.start()
        cp.wait()
        across = xg.at[pl.ds(pl.multiple_of(2 * ROWS + r * PR + c * HR, HR), HR), :]
        xs["p", r] = remote(mine, across, x_send.at[r], x_recv.at[r], par)
        xs["p", r].start()
        xs["s", r] = remote(mine, xg.at[pl.ds(ROWS + r * HR, HR), :], x_send.at[4 + r], x_recv.at[4 + r], sib)
        xs["s", r].start()

    def forward_x(r):
        xs["p", r].wait_recv()
        across = xg.at[pl.ds(pl.multiple_of(2 * ROWS + r * PR + c * HR, HR), HR), :]
        xs["f", r] = remote(across, across, x_send.at[8 + r], x_recv.at[8 + r], sib)
        xs["f", r].start()

    def h_tiles(n, p_of, j_of):
        def load(t, s):
            rows = pl.ds(pl.multiple_of(p_of(t) * PR, PR), PR)
            return pltpu.make_async_copy(xg.at[rows, :], xbuf.at[s], l_sem.at[s])

        def store(t, s):
            rows = pl.ds(pl.multiple_of(p_of(t) * PR, PR), PR)
            cols = pl.ds(pl.multiple_of(j_of(t) * CW, CW), CW)
            return pltpu.make_async_copy(hbuf.at[s], hg.at[rows, cols], l_sem.at[2 + s])

        load(0, 0).start()

        @pl.loop(0, n)
        def _(t):
            s = t % 2

            @pl.when(t + 1 < n)
            def _():
                load(t + 1, (t + 1) % 2).start()

            load(t, s).wait()

            @pl.when(t >= 2)
            def _():
                store(t, s).wait()

            j = j_of(t)

            @pl.loop(0, PR // HR)
            def _(r):
                rows = pl.ds(pl.multiple_of(r * HR, HR), HR)
                acc = jnp.dot(xbuf[s, rows, :], w1v[j], preferred_element_type=F32)
                hbuf[s, rows, :] = jax.nn.gelu(acc, approximate=True).astype(BF16)

            store(t, s).start()

        if n >= 2:
            store(n - 2, (n - 2) % 2).wait()
        store(n - 1, (n - 1) % 2).wait()

    def own_tiles(j):
        h_tiles(4, lambda t: t, lambda t: j)

    def got_x(r):
        xs["f", r].wait_recv()

    for t in range(NC + 2):
        if t >= 2:
            s3_ready = t - 2
        if t - 1 >= 0 and t - 1 < NC:
            s2(t - 1)
        if t < NC:
            s1(t)
            if t + 3 < NC:
                s0(t + 3)
        if t == NC - 1:
            for m in (0, 1, 2):
                w2m[m].start()
        if t in (1, 3, 5):
            forward_x(t // 2)
        if t == NC + 1:
            forward_x(3)
        if t >= 2:
            s3(s3_ready)
            if t == 2:
                for r in range(4):
                    xs["s", r].wait_recv()
            own_tiles(s3_ready)
        if t == 3:
            got_x(0)
            h_tiles(2, lambda n: 4, lambda n: n)
        if t == 4:
            h_tiles(1, lambda n: 4, lambda n: 2)
        if t == 5:
            got_x(1)
            h_tiles(5, lambda n: 4 + (n + 3) // 4, lambda n: (n + 3) % 4)
        if t == 6:
            got_x(2)
            h_tiles(5, lambda n: 4 + n // 2 - n // 4 + (n // 4) * 1, lambda n: 4) if False else h_tiles(2, lambda n: 4 + n, lambda n: 4)
            h_tiles(3, lambda n: 6, lambda n: n)
        if t == 7:
            h_tiles(2, lambda n: 4 + n, lambda n: 5)
            h_tiles(3, lambda n: 6, lambda n: 3 + n)
        if t == 8:
            got_x(3)
            h_tiles(3, lambda n: 4 + n, lambda n: 6)
            h_tiles(7, lambda n: 7, lambda n: n)

    def h_load(p, s):
        rows = pl.ds(pl.multiple_of(p * PR, PR), PR)
        return pltpu.make_async_copy(hg.at[rows, :], xbuf.at[s, :, pl.ds(0, FS)], l_sem.at[s])

    def col_of(kk):
        g = (kk + 1) // 3
        nz = (g + 1) // 2
        dz = nz * (kk % 3 + 1)
        dy = (1 - nz) * kk + g // 2
        return ((z + dz) % 4) * 2 + (yq + dy) % 2

    def dd_msg(n, s):
        return remote(ubuf.at[s, 1 - c], d2d.at[n], dd_send.at[s], dd_recv.at[n], sib)

    def rs_msg(n):
        return remote(sbuf.at[n], rs.at[n], rs_send.at[n], rs_recv.at[n], par)

    def sp_msg(n, s):
        return remote(tbuf.at[s], sibp.at[n], sp_send.at[s], sp_recv.at[n], sib)

    def pass_on(n, s):
        dd_msg(n, s).wait_recv()
        cp = pltpu.make_async_copy(d2d.at[n], dbuf, l_sem.at[2])
        cp.start()
        cp.wait()
        stage[...] = ubuf[s, c] + dbuf[...]
        cp = pltpu.make_async_copy(stage, sbuf.at[n], l_sem.at[2])
        cp.start()
        cp.wait()
        rs_msg(n).start()
        dd_msg(n, s).wait_send()

    def finish(kk, col, last):
        for p in range(2):
            h_load(p, p).start()
        cols = pl.ds(pl.multiple_of(col * KB, KB), KB)
        for p in range(2):
            h_load(p, p).wait()
            rows = pl.ds(p * PR, PR)
            n = kk * 2 + p
            sp_msg(n, p).wait_recv()
            cx = pltpu.make_async_copy(x_ref.at[rows, cols], xtv, l_sem.at[2])
            cx.start()
            cs = pltpu.make_async_copy(sibp.at[n], sibv, l_sem.at[3])
            cs.start()

            @pl.loop(0, PR // HR)
            def _(r):
                rr = pl.ds(pl.multiple_of(r * HR, HR), HR)
                tbuf[p, rr, :] = jnp.dot(xbuf[p, rr, pl.ds(0, FS)], wbuf[...], preferred_element_type=F32)

            cs.wait()
            cx.wait()

            @pl.loop(0, 2)
            def _(r):
                rr = pl.ds(pl.multiple_of(r * HR, HR), HR)
                m = kk * 4 + p * 2 + r
                rs_msg(m).wait_recv()
                cr = pltpu.make_async_copy(rs.at[m], rsv, l_sem.at[2])
                cr.start()
                cr.wait()
                total = tbuf[p, rr, :] + sibv[rr, :] + rsv[...]
                obuf[rr, :] = (xtv[rr, :].astype(F32) + total).astype(BF16)

            co = pltpu.make_async_copy(obuf, y_ref.at[rows, cols], l_sem.at[2])
            co.start()
            co.wait()

    def w2_load(kk):
        @pl.when(kk == 0)
        def _():
            cp = pltpu.make_async_copy(w2_ref, wbuf, l_sem.at[2])
            cp.start()
            cp.wait()

        @pl.when(kk > 0)
        def _():
            cp = pltpu.make_async_copy(w2g.at[col_of(kk)], wbuf, l_sem.at[2])
            cp.start()
            cp.wait()

    def own_part(kk):
        w2_load(kk)
        finish(kk, col_of(kk), False)

    @pl.loop(0, 9)
    def _(kk):
        @pl.when(kk == 1)
        def _():
            for m in (1, 2, 0):
                w2m[m].wait_recv()
            for m in (3, 4, 5, 6):
                w2m[m].start()

        @pl.when(kk == 4)
        def _():
            w2m[3].wait_recv()
            w2m[4].wait_recv()
            w2m[7].start()

        @pl.when(kk == 5)
        def _():
            w2m[5].wait_recv()

        @pl.when(kk == 6)
        def _():
            w2m[6].wait_recv()

        @pl.when(kk == 7)
        def _():
            w2m[7].wait_recv()

        @pl.when(kk < 8)
        def _():
            w2_load(kk)
            h_load(4, 0).start()

            @pl.loop(0, 4)
            def _(q):
                s = q % 2

                @pl.when(q < 3)
                def _():
                    h_load(5 + q, 1 - s).start()

                h_load(4 + q, s).wait()

                @pl.loop(0, 2)
                def _(r):
                    rr = pl.ds(pl.multiple_of(r * HR, HR), HR)
                    ubuf[s, r] = jnp.dot(xbuf[s, rr, pl.ds(0, FS)], wbuf[...], preferred_element_type=F32)

                dd_msg(kk * 4 + q, s).start()

                @pl.when(q > 0)
                def _():
                    pass_on(kk * 4 + q - 1, 1 - s)

            pass_on(kk * 4 + 3, 1)

            h_load(2, 0).start()
            h_load(3, 1).start()

            @pl.loop(0, 2)
            def _(p):
                h_load(2 + p, p).wait()

                @pl.loop(0, PR // HR)
                def _(r):
                    rr = pl.ds(pl.multiple_of(r * HR, HR), HR)
                    tbuf[p, rr, :] = jnp.dot(xbuf[p, rr, pl.ds(0, FS)], wbuf[...], preferred_element_type=F32)

                sp_msg(kk * 2 + p, p).start()

            for p in range(2):
                sp_msg(kk * 2 + p, p).wait_send()

        @pl.when(kk > 0)
        def _():
            own_part(kk - 1)

    for cp in sends.values():
        cp.wait_send()
    for cp in w2m:
        cp.wait_send()
    for cp in xs.values():
        cp.wait_send()

    @pl.loop(0, 32)
    def _(n):
        rs_msg(n).wait_send()


def _block(x, gamma, w1, w2):
    hbm = pl.BlockSpec(memory_space=pl.ANY)
    out = pl.pallas_call(
        _kernel,
        name="mlp",
        out_shape=[
            jax.ShapeDtypeStruct((ROWS, D), BF16),
            jax.ShapeDtypeStruct((4 * ROWS, D), BF16),
            jax.ShapeDtypeStruct((4 * ROWS, FS), BF16),
            jax.ShapeDtypeStruct((8, FS, KB), BF16),
            jax.ShapeDtypeStruct((32, HR, KB), F32),
            jax.ShapeDtypeStruct((32, HR, KB), F32),
            jax.ShapeDtypeStruct((32, HR, KB), F32),
            jax.ShapeDtypeStruct((16, PR, KB), F32),
        ],
        in_specs=[hbm, pl.BlockSpec(memory_space=pltpu.VMEM), hbm, hbm],
        out_specs=[hbm] * 8,
        scratch_shapes=[
            pltpu.VMEM((NC, D, CW), BF16),
            pltpu.VMEM((2, PR, D), BF16),
            pltpu.VMEM((2, PR, CW), BF16),
            pltpu.VMEM((FS, KB), BF16),
            pltpu.VMEM((2, 2, HR, KB), F32),
            pltpu.VMEM((HR, KB), F32),
            pltpu.VMEM((HR, KB), F32),
            pltpu.VMEM((2, PR, KB), F32),
            pltpu.VMEM((PR, KB), F32),
            pltpu.VMEM((HR, KB), F32),
            pltpu.VMEM((PR, KB), BF16),
            pltpu.VMEM((PR, KB), BF16),
            pltpu.SemaphoreType.DMA((NC, 9)),
            pltpu.SemaphoreType.DMA((NC, 9)),
            pltpu.SemaphoreType.DMA((8,)),
            pltpu.SemaphoreType.DMA((8,)),
            pltpu.SemaphoreType.DMA((12,)),
            pltpu.SemaphoreType.DMA((12,)),
            pltpu.SemaphoreType.DMA((2,)),
            pltpu.SemaphoreType.DMA((32,)),
            pltpu.SemaphoreType.DMA((32,)),
            pltpu.SemaphoreType.DMA((32,)),
            pltpu.SemaphoreType.DMA((2,)),
            pltpu.SemaphoreType.DMA((16,)),
            pltpu.SemaphoreType.DMA((4,)),
            pltpu.SemaphoreType.DMA((NC,)),
        ],
        compiler_params=pltpu.CompilerParams(
            collective_id=0, has_side_effects=True, vmem_limit_bytes=67000000
        ),
    )(x, gamma.reshape(1, D), w1, w2)
    return out[0]


def solution(mesh):
    return jax.shard_map(
        _block,
        mesh=mesh,
        in_specs=(P(("fsdp", "tp"), None), P(None), P("fsdp", "tp"), P("tp", "fsdp")),
        out_specs=P(("fsdp", "tp"), None),
        check_vma=False,
    )
```

time: 1950 us -> 979 us (0.50)
  waiting for transfers between devices: 1630 us -> 0 us
  Pallas kernels: 0 us -> 968 us
  matrix products: 277 us -> 0 us
  other arithmetic: 33.6 us -> 0 us
    all_gather x3 -> x0, waiting for transfers between devices: 1180 us -> none  [the longest x1 553 us: body(): w1f = lax.all_gather(w1, 'fsdp', axis=0, tiled=True)]
    pallas_call x0 -> x1, Pallas kernels: none -> 968 us  [_block(): pl.pallas_call(_kernel, name='mlp', out_shape=[jax.ShapeDtypeStruct((ROWS...]
    unnamed x5 -> x0, waiting for transfers between devices: 451 us -> none
    dot_general x2 -> x0, matrix products: 277 us -> none  [the longest x1 143 us: body(): yp = jnp.dot(h, w2f, preferred_element_type=jnp.float32)]
    convert_element_type x2 -> x0, other arithmetic: 23.4 us -> none  [the longest x1 12 us: body(): return (xf + y).astype(jnp.bfloat16)]
  transfers between devices with their start and end apart: 4 -> 0, of which waited for: 4 -> 0; matrix products, arithmetic and copies ran while one was open for 7% -> 0% of each run, Pallas kernels for 0% -> 0%
where the time goes in v1:
time: 979 us; the launch traced here: 975 us
  Pallas kernels  968 us (99%)
    pallas_call x1, Pallas kernels, _block(): pl.pallas_call(_kernel, name='mlp', out_shape=[jax.ShapeDtypeStruct((ROWS...  968 us

profile of v1, /device:TPU:0, one launch (start us, length us, event | category | flops | bytes accessed | tf_op | source)
XLA Modules:
  0.0 975.5 jit_solution(2259504518175250330)
XLA Ops:
  0.0 967.6 %mlp.1 = (bf16[1024,4096]{1,0:T(8,128)(2,1)}, bf16[4096,4096]{1,0:T(8,128)(2,1)}, bf16[4096,3584]{1,0:T(8,128)(2,1)}, bf16[8,3584,512]{2,1,0:T(8,128)(2,1)}, f32...) custom-call(bf16[1024,4096]{1,0:T(8,128)(2,1)} %x_ref.1, ...), custom_call_target="tpu_custom_call" | custom-call | tf_op jit(solution)/shard_map/mlp/pallas_call | solution.py:431
  967.6 7.9 copy.6

commit v2 on v1

--- a/solution.py
+++ b/solution.py
@@ -19,6 +19,8 @@
 KB = D // 8
 PR = 512
 HR = PR // 2
+CUT1 = KB * 27 // 32
+CUT2 = FS * 27 // 32
 
 
 def _kernel(
@@ -32,10 +34,9 @@
     a, b = lax.axis_index("fsdp"), lax.axis_index("tp")
     z, yq = a // 2, a % 2
     c = b % 2
-    zp, zm, z2 = ((z + 1) % 4) * 2 + yq, ((z + 3) % 4) * 2 + yq, ((z + 2) % 4) * 2 + yq
-    yy = z * 2 + (1 - yq)
-    zpy, zmy, z2y = ((z + 1) % 4) * 2 + 1 - yq, ((z + 3) % 4) * 2 + 1 - yq, ((z + 2) % 4) * 2 + 1 - yq
-    to_zp, to_zm, to_yy = (zp, b), (zm, b), (yy, b)
+    to_zp = (lax.rem(z + 1, 4) * 2 + yq, b)
+    to_zm = (lax.rem(z + 3, 4) * 2 + yq, b)
+    to_yy = (z * 2 + 1 - yq, b)
     sib = (a, (b // 2) * 2 + 1 - c)
     par = (a, (1 - b // 2) * 2 + c)
 
@@ -49,85 +50,107 @@
             src_ref=src, dst_ref=dst, send_sem=ssem, recv_sem=rsem, device_id=dev, device_id_type=MESH
         )
 
-    sends = {}
-
-    def w1_reg(j, s, lo, n):
-        return w1v.at[j, pl.ds(pl.multiple_of(s * KB + lo, HR), n), :]
-
-    def w1_msg(j, m, dev, s, lo=0, n=KB, own=False):
-        dst = w1_reg(j, s, lo, n)
-        src = w1_ref.at[:, pl.ds(j * CW, CW)] if own else dst
-        cp = remote(src, dst, w1_send.at[j, m], w1_recv.at[j, m], dev)
-        cp.start()
-        sends[(j, m)] = cp
-
-    def w1_got(j, m):
-        sends[(j, m)].wait_recv()
-
+    def messages(reg, own, send, recv, n, cut):
+        m = {}
+
+        def blk(dz, dy):
+            return (z + dz) * 2 + (1 - yq if dy else yq)
+
+        def add(key, dev, dz, dy, lo, cnt, sent, got, first=False):
+            i = len(m)
+            dst = reg(blk(dz, dy), lo, cnt)
+            m[key] = (remote(own if first else dst, dst, send(i), recv(i), dev), sent, got)
+
+        always = None
+        add("Y0", to_yy, 0, 0, 0, n, always, always, True)
+        for d in (1, 2, 3):
+            right = (z <= 2) & (z >= d - 1)
+            left = (z >= 1) & (z <= 4 - d)
+            add(("R", d), to_zp, 1 - d, 0, 0, n, right, z >= d, d == 1)
+            add(("L", d), to_zm, d - 1, 0, 0, n, left, z <= 3 - d, d == 1)
+            add(("YL", d), to_yy, -d, 0, 0, cut, z >= d, z >= d)
+            add(("YR", d), to_yy, d, 0, 0, cut, z <= 3 - d, z <= 3 - d)
+            add(("BR", d), to_zp, 1 - d, 1, cut, n - cut, right, z >= d)
+            add(("BL", d), to_zm, d - 1, 1, cut, n - cut, left, z <= 3 - d)
+        return m
+
+    def when(cond, f):
+        if cond is None:
+            f()
+        else:
+            pl.when(cond)(f)
+
+    def send(m, *keys):
+        for k in keys:
+            when(m[k][1], m[k][0].start)
+
+    def got(m, *keys):
+        for k in keys:
+            when(m[k][2], m[k][0].wait_recv)
+
+    def stage0(m):
+        send(m, "Y0", ("R", 1), ("L", 1))
+
+    def stage1(m):
+        got(m, ("R", 1), ("L", 1))
+        send(m, ("R", 2), ("L", 2), ("YL", 1), ("YR", 1))
+        got(m, "Y0")
+        send(m, ("BR", 1), ("BL", 1))
+
+    def stage2(m):
+        got(m, ("R", 2), ("L", 2))
+        send(m, ("R", 3), ("L", 3), ("YL", 2), ("YR", 2))
+        got(m, ("BR", 1), ("BL", 1))
+        send(m, ("BR", 2), ("BL", 2))
+
+    def stage3(m):
+        got(m, ("R", 3), ("L", 3))
+        send(m, ("YL", 3), ("YR", 3))
+        got(m, ("BR", 2), ("BL", 2))
+        send(m, ("BR", 3), ("BL", 3))
+
+    def stage4(m):
+        for d in (1, 2, 3):
+            got(m, ("YL", d), ("YR", d))
+        got(m, ("BR", 3), ("BL", 3))
+
+    def w1_messages(j):
+        def reg(s, lo, n):
+            return w1v.at[j, pl.ds(pl.multiple_of(s * KB + lo, 16), n), :]
+
+        own = w1_ref.at[:, pl.ds(pl.multiple_of(j * CW, CW), CW)]
+        return messages(reg, own, lambda i: w1_send.at[j, i], lambda i: w1_recv.at[j, i], KB, CUT1)
+
+    w1m = [w1_messages(j) for j in range(NC)]
     loc = {}
 
     def s0(j):
-        w1_msg(j, 0, to_yy, a, own=True)
-        w1_msg(j, 1, to_zp, a, own=True)
-        w1_msg(j, 2, to_zm, a, own=True)
-        cp = pltpu.make_async_copy(w1_ref.at[:, pl.ds(j * CW, CW)], w1_reg(j, a, 0, KB), loc_sem.at[j])
+        stage0(w1m[j])
+        dst = w1v.at[j, pl.ds(pl.multiple_of(a * KB, KB), KB), :]
+        cp = pltpu.make_async_copy(w1_ref.at[:, pl.ds(j * CW, CW)], dst, loc_sem.at[j])
         cp.start()
         loc[j] = cp
 
     def s1(j):
-        w1_got(j, 0)
-        if j % 2 == 0:
-            w1_msg(j, 3, to_zp, yy)
-            w1_msg(j, 4, to_zm, yy)
-        w1_got(j, 1)
-        w1_got(j, 2)
-        w1_msg(j, 5, to_zp, zm, 0, HR)
-        w1_msg(j, 6, to_zm, zp, HR, HR)
-        if j % 2 == 1:
-            w1_msg(j, 3, to_yy, zm)
-            w1_msg(j, 4, to_yy, zp)
+        stage1(w1m[j])
 
     def s2(j):
-        if j % 2 == 0:
-            w1_got(j, 3)
-            w1_msg(j, 7, to_zp, zmy, 0, HR)
-            w1_got(j, 4)
-            w1_msg(j, 8, to_zm, zpy, HR, HR)
-            w1_got(j, 5)
-            w1_got(j, 6)
-        else:
-            w1_got(j, 5)
-            w1_got(j, 6)
-            w1_msg(j, 7, to_yy, z2)
-            w1_got(j, 3)
-            w1_got(j, 4)
+        stage2(w1m[j])
 
     def s3(j):
-        w1_got(j, 7)
-        if j % 2 == 0:
-            w1_got(j, 8)
+        stage3(w1m[j])
+
+    def s4(j):
+        stage4(w1m[j])
         loc[j].wait()
 
-    def w2_msg(m, dev, s, lo=0, n=FS, own=False):
-        dst = w2g.at[s, pl.ds(lo, n), :]
-        src = w2_ref if own else dst
-        return remote(src, dst, w2_send.at[m], w2_recv.at[m], dev)
-
-    H2 = FS // 2
-    w2m = [
-        w2_msg(0, to_yy, a, own=True),
-        w2_msg(1, to_zp, a, own=True),
-        w2_msg(2, to_zm, a, own=True),
-        w2_msg(3, to_zp, zm, 0, H2),
-        w2_msg(4, to_zm, zp, H2, H2),
-        w2_msg(5, to_yy, zm),
-        w2_msg(6, to_yy, zp),
-        w2_msg(7, to_yy, z2),
-    ]
+    w2m = messages(
+        lambda s, lo, n: w2g.at[s, pl.ds(lo, n), :],
+        w2_ref, lambda i: w2_send.at[i], lambda i: w2_recv.at[i], FS, CUT2,
+    )
 
     s0(0)
     s0(1)
-    s0(2)
 
     def x_in(r):
         return pltpu.make_async_copy(x_ref.at[pl.ds(r * HR, HR), :], xbuf.at[r % 2, pl.ds(0, HR), :], l_sem.at[r % 2])
@@ -210,58 +233,49 @@
     def got_x(r):
         xs["f", r].wait_recv()
 
-    for t in range(NC + 2):
-        if t >= 2:
-            s3_ready = t - 2
-        if t - 1 >= 0 and t - 1 < NC:
+    for t in range(NC + 3):
+        if 0 <= t - 2 < NC:
+            s3(t - 2)
+        if 0 <= t - 1 < NC:
             s2(t - 1)
         if t < NC:
             s1(t)
-            if t + 3 < NC:
-                s0(t + 3)
-        if t == NC - 1:
-            for m in (0, 1, 2):
-                w2m[m].start()
-        if t in (1, 3, 5):
-            forward_x(t // 2)
+        if t + 2 < NC:
+            s0(t + 2)
         if t == NC + 1:
-            forward_x(3)
-        if t >= 2:
-            s3(s3_ready)
-            if t == 2:
-                for r in range(4):
-                    xs["s", r].wait_recv()
-            own_tiles(s3_ready)
+            stage0(w2m)
+        if 2 <= t < 6:
+            forward_x(t - 2)
+        if t < 3:
+            continue
+        j = t - 3
+        s4(j)
         if t == 3:
-            got_x(0)
-            h_tiles(2, lambda n: 4, lambda n: n)
-        if t == 4:
-            h_tiles(1, lambda n: 4, lambda n: 2)
-        if t == 5:
-            got_x(1)
-            h_tiles(5, lambda n: 4 + (n + 3) // 4, lambda n: (n + 3) % 4)
-        if t == 6:
-            got_x(2)
-            h_tiles(5, lambda n: 4 + n // 2 - n // 4 + (n // 4) * 1, lambda n: 4) if False else h_tiles(2, lambda n: 4 + n, lambda n: 4)
-            h_tiles(3, lambda n: 6, lambda n: n)
-        if t == 7:
-            h_tiles(2, lambda n: 4 + n, lambda n: 5)
-            h_tiles(3, lambda n: 6, lambda n: 3 + n)
-        if t == 8:
-            got_x(3)
-            h_tiles(3, lambda n: 4 + n, lambda n: 6)
-            h_tiles(7, lambda n: 7, lambda n: n)
+            for r in range(4):
+                xs["s", r].wait_recv()
+        if j < 4:
+            own_tiles(j)
+            got_x(j)
+            if j > 0:
+                h_tiles(j, lambda n: 4 + n, lambda n: j)
+            h_tiles(j + 1, lambda n: 4 + j, lambda n: n)
+        else:
+            h_tiles(4, lambda n: 4 + n, lambda n: j)
 
     def h_load(p, s):
         rows = pl.ds(pl.multiple_of(p * PR, PR), PR)
         return pltpu.make_async_copy(hg.at[rows, :], xbuf.at[s, :, pl.ds(0, FS)], l_sem.at[s])
 
+    def pick(kk, values):
+        return sum(jnp.where(kk == k, v, 0) for k, v in enumerate(values) if v)
+
     def col_of(kk):
-        g = (kk + 1) // 3
-        nz = (g + 1) // 2
-        dz = nz * (kk % 3 + 1)
-        dy = (1 - nz) * kk + g // 2
-        return ((z + dz) % 4) * 2 + (yq + dy) % 2
+        i = pick(kk, (0, 0, 1, 2, 1, 3, 2, 3))
+        dy = pick(kk, (0, 1, 0, 0, 1, 0, 1, 1))
+        e = jnp.where(z < 2, z, 3 - z)
+        v = jnp.where(i <= e, i - 1, i)
+        v = jnp.where(z < 2, v, 3 - v)
+        return jnp.where(i == 0, z, v) * 2 + lax.rem(yq + dy, 2)
 
     def dd_msg(n, s):
         return remote(ubuf.at[s, 1 - c], d2d.at[n], dd_send.at[s], dd_recv.at[n], sib)
@@ -342,28 +356,25 @@
     def _(kk):
         @pl.when(kk == 1)
         def _():
-            for m in (1, 2, 0):
-                w2m[m].wait_recv()
-            for m in (3, 4, 5, 6):
-                w2m[m].start()
-
-        @pl.when(kk == 4)
-        def _():
-            w2m[3].wait_recv()
-            w2m[4].wait_recv()
-            w2m[7].start()
+            stage1(w2m)
+
+        @pl.when(kk == 3)
+        def _():
+            stage2(w2m)
+            got(w2m, ("YL", 1), ("YR", 1))
 
         @pl.when(kk == 5)
         def _():
-            w2m[5].wait_recv()
+            stage3(w2m)
+            got(w2m, ("YL", 2), ("YR", 2))
 
         @pl.when(kk == 6)
         def _():
-            w2m[6].wait_recv()
+            got(w2m, ("BR", 3), ("BL", 3))
 
         @pl.when(kk == 7)
         def _():
-            w2m[7].wait_recv()
+            got(w2m, ("YL", 3), ("YR", 3))
 
         @pl.when(kk < 8)
         def _():
@@ -393,6 +404,10 @@
 
             pass_on(kk * 4 + 3, 1)
 
+            @pl.when(kk == 0)
+            def _():
+                h_tiles(12, lambda n: n % 4, lambda n: 4 + n // 4)
+
             h_load(2, 0).start()
             h_load(3, 1).start()
 
@@ -414,10 +429,9 @@
         def _():
             own_part(kk - 1)
 
-    for cp in sends.values():
-        cp.wait_send()
-    for cp in w2m:
-        cp.wait_send()
+    for m in (*w1m, w2m):
+        for cp, sent, _ in m.values():
+            when(sent, cp.wait_send)
     for cp in xs.values():
         cp.wait_send()
 
@@ -456,10 +470,10 @@
             pltpu.VMEM((HR, KB), F32),
             pltpu.VMEM((PR, KB), BF16),
             pltpu.VMEM((PR, KB), BF16),
-            pltpu.SemaphoreType.DMA((NC, 9)),
-            pltpu.SemaphoreType.DMA((NC, 9)),
-            pltpu.SemaphoreType.DMA((8,)),
-            pltpu.SemaphoreType.DMA((8,)),
+            pltpu.SemaphoreType.DMA((NC, 19)),
+            pltpu.SemaphoreType.DMA((NC, 19)),
+            pltpu.SemaphoreType.DMA((19,)),
+            pltpu.SemaphoreType.DMA((19,)),
             pltpu.SemaphoreType.DMA((12,)),
             pltpu.SemaphoreType.DMA((12,)),
             pltpu.SemaphoreType.DMA((2,)),

time: 979 us -> 759 us (0.78)
  the two profiles are of different devices: /device:TPU:0 before, /device:TPU:18 now
where the time goes in v2:
time: 759 us; the launch traced here: 755 us
  Pallas kernels  747 us (98%)
  local copies, waits for them, and re-layouts  7.89 us (1%)
    pallas_call x1, Pallas kernels, _block(): pl.pallas_call(_kernel, name='mlp', out_shape=[jax.ShapeDtypeStruct((ROWS...  747 us

profile of v2, /device:TPU:18, one launch (start us, length us, event | category | flops | bytes accessed | tf_op | source)
XLA Modules:
  0.0 754.7 jit_solution(11532669024480718644)
XLA Ops:
  0.0 746.8 %mlp.1 = (bf16[1024,4096]{1,0:T(8,128)(2,1)}, bf16[4096,4096]{1,0:T(8,128)(2,1)}, bf16[4096,3584]{1,0:T(8,128)(2,1)}, bf16[8,3584,512]{2,1,0:T(8,128)(2,1)}, f32...) custom-call(bf16[1024,4096]{1,0:T(8,128)(2,1)} %x_ref.1, ...), custom_call_target="tpu_custom_call" | custom-call | tf_op jit(solution)/shard_map/mlp/pallas_call | solution.py:445
  746.8 7.9 %copy.6 = bf16[1024,4096]{1,0:T(8,128)(2,1)} copy(bf16[1024,4096]{1,0:T(8,128)(2,1)} %get-tuple-element.6) | data formatting | bytes 16777216

commit v3 on v2

--- a/solution.py
+++ b/solution.py
@@ -19,6 +19,8 @@
 KB = D // 8
 PR = 512
 HR = PR // 2
+LEAD2 = 512
+HC = CW // 2
 CUT1 = KB * 27 // 32
 CUT2 = FS * 27 // 32
 
@@ -26,10 +28,10 @@
 def _kernel(
     x_ref, gamma_ref, w1_ref, w2_ref,
     y_ref, xg, hg, w2g, d2d, sbuf, rs, sibp,
-    w1v, xbuf, hbuf, wbuf, ubuf, dbuf, stage, tbuf, sibv, rsv, xtv, obuf,
+    w1v, xbuf, hbuf, wbuf, ubuf, dbuf, stage, tbuf, ybuf, sibv, rsv, xtv, obuf,
     w1_send, w1_recv, w2_send, w2_recv, x_send, x_recv,
     dd_send, dd_recv, rs_send, rs_recv, sp_send, sp_recv,
-    l_sem, loc_sem,
+    l_sem, loc_sem, w_sem, o_sem,
 ):
     a, b = lax.axis_index("fsdp"), lax.axis_index("tp")
     z, yq = a // 2, a % 2
@@ -50,7 +52,7 @@
             src_ref=src, dst_ref=dst, send_sem=ssem, recv_sem=rsem, device_id=dev, device_id_type=MESH
         )
 
-    def messages(reg, own, send, recv, n, cut):
+    def messages(reg, own, send, recv, n, cut, lead):
         m = {}
 
         def blk(dz, dy):
@@ -59,15 +61,19 @@
         def add(key, dev, dz, dy, lo, cnt, sent, got, first=False):
             i = len(m)
             dst = reg(blk(dz, dy), lo, cnt)
-            m[key] = (remote(own if first else dst, dst, send(i), recv(i), dev), sent, got)
+            m[key] = (remote(own(lo, cnt) if first else dst, dst, send(i), recv(i), dev), sent, got)
 
         always = None
         add("Y0", to_yy, 0, 0, 0, n, always, always, True)
         for d in (1, 2, 3):
             right = (z <= 2) & (z >= d - 1)
             left = (z >= 1) & (z <= 4 - d)
-            add(("R", d), to_zp, 1 - d, 0, 0, n, right, z >= d, d == 1)
-            add(("L", d), to_zm, d - 1, 0, 0, n, left, z <= 3 - d, d == 1)
+            skip = lead if d == 1 else 0
+            if skip:
+                add(("R", 0), to_zp, 0, 0, 0, skip, right, z >= 1, True)
+                add(("L", 0), to_zm, 0, 0, 0, skip, left, z <= 2, True)
+            add(("R", d), to_zp, 1 - d, 0, skip, n - skip, right, z >= d, d == 1)
+            add(("L", d), to_zm, d - 1, 0, skip, n - skip, left, z <= 3 - d, d == 1)
             add(("YL", d), to_yy, -d, 0, 0, cut, z >= d, z >= d)
             add(("YR", d), to_yy, d, 0, 0, cut, z <= 3 - d, z <= 3 - d)
             add(("BR", d), to_zp, 1 - d, 1, cut, n - cut, right, z >= d)
@@ -118,8 +124,10 @@
         def reg(s, lo, n):
             return w1v.at[j, pl.ds(pl.multiple_of(s * KB + lo, 16), n), :]
 
-        own = w1_ref.at[:, pl.ds(pl.multiple_of(j * CW, CW), CW)]
-        return messages(reg, own, lambda i: w1_send.at[j, i], lambda i: w1_recv.at[j, i], KB, CUT1)
+        def own(lo, n):
+            return w1_ref.at[pl.ds(lo, n), pl.ds(j * CW, CW)]
+
+        return messages(reg, own, lambda i: w1_send.at[j, i], lambda i: w1_recv.at[j, i], KB, CUT1, 0)
 
     w1m = [w1_messages(j) for j in range(NC)]
     loc = {}
@@ -146,7 +154,8 @@
 
     w2m = messages(
         lambda s, lo, n: w2g.at[s, pl.ds(lo, n), :],
-        w2_ref, lambda i: w2_send.at[i], lambda i: w2_recv.at[i], FS, CUT2,
+        lambda lo, n: w2_ref.at[pl.ds(lo, n), :],
+        lambda i: w2_send.at[i], lambda i: w2_recv.at[i], FS, CUT2, LEAD2,
     )
 
     s0(0)
@@ -227,9 +236,6 @@
             store(n - 2, (n - 2) % 2).wait()
         store(n - 1, (n - 1) % 2).wait()
 
-    def own_tiles(j):
-        h_tiles(4, lambda t: t, lambda t: j)
-
     def got_x(r):
         xs["f", r].wait_recv()
 
@@ -242,25 +248,33 @@
             s1(t)
         if t + 2 < NC:
             s0(t + 2)
+        if t == NC:
+            send(w2m, ("R", 0), ("L", 0))
         if t == NC + 1:
             stage0(w2m)
-        if 2 <= t < 6:
-            forward_x(t - 2)
+        if t in (1, 2):
+            forward_x(t - 1)
         if t < 3:
             continue
         j = t - 3
         s4(j)
-        if t == 3:
+        if j == 0:
             for r in range(4):
                 xs["s", r].wait_recv()
-        if j < 4:
-            own_tiles(j)
-            got_x(j)
-            if j > 0:
-                h_tiles(j, lambda n: 4 + n, lambda n: j)
-            h_tiles(j + 1, lambda n: 4 + j, lambda n: n)
-        else:
+            got_x(0)
+        if j < 3:
+            got_x(j + 1)
+            h_tiles(
+                6 + 2 * j,
+                lambda n: jnp.minimum(n, 5 + j),
+                lambda n: jnp.where(n < 5 + j, j, n - 5 - j),
+            )
+        elif j == 3:
+            h_tiles(8, lambda n: n, lambda n: j)
+        elif j < NC - 1:
             h_tiles(4, lambda n: 4 + n, lambda n: j)
+        if j < 2:
+            forward_x(j + 2)
 
     def h_load(p, s):
         rows = pl.ds(pl.multiple_of(p * PR, PR), PR)
@@ -270,8 +284,8 @@
         return sum(jnp.where(kk == k, v, 0) for k, v in enumerate(values) if v)
 
     def col_of(kk):
-        i = pick(kk, (0, 0, 1, 2, 1, 3, 2, 3))
-        dy = pick(kk, (0, 1, 0, 0, 1, 0, 1, 1))
+        i = pick(kk, (0, 1, 0, 2, 1, 3, 2, 3))
+        dy = pick(kk, (0, 0, 1, 0, 1, 0, 1, 1))
         e = jnp.where(z < 2, z, 3 - z)
         v = jnp.where(i <= e, i - 1, i)
         v = jnp.where(z < 2, v, 3 - v)
@@ -286,148 +300,232 @@
     def sp_msg(n, s):
         return remote(tbuf.at[s], sibp.at[n], sp_send.at[s], sp_recv.at[n], sib)
 
-    def pass_on(n, s):
+    def d2d_in(n):
+        return pltpu.make_async_copy(d2d.at[n], dbuf, l_sem.at[2])
+
+    def sum_out(n):
+        return pltpu.make_async_copy(stage, sbuf.at[n], l_sem.at[3])
+
+    def pass_start(n, s):
         dd_msg(n, s).wait_recv()
-        cp = pltpu.make_async_copy(d2d.at[n], dbuf, l_sem.at[2])
-        cp.start()
-        cp.wait()
+        d2d_in(n).start()
+
+    def pass_sum(n, s):
+        d2d_in(n).wait()
         stage[...] = ubuf[s, c] + dbuf[...]
-        cp = pltpu.make_async_copy(stage, sbuf.at[n], l_sem.at[2])
-        cp.start()
-        cp.wait()
+        sum_out(n).start()
+        dd_msg(n, s).wait_send()
+
+    def pass_send(n):
+        sum_out(n).wait()
         rs_msg(n).start()
-        dd_msg(n, s).wait_send()
-
-    def finish(kk, col, last):
-        for p in range(2):
-            h_load(p, p).start()
-        cols = pl.ds(pl.multiple_of(col * KB, KB), KB)
-        for p in range(2):
-            h_load(p, p).wait()
-            rows = pl.ds(p * PR, PR)
-            n = kk * 2 + p
-            sp_msg(n, p).wait_recv()
-            cx = pltpu.make_async_copy(x_ref.at[rows, cols], xtv, l_sem.at[2])
-            cx.start()
-            cs = pltpu.make_async_copy(sibp.at[n], sibv, l_sem.at[3])
-            cs.start()
-
-            @pl.loop(0, PR // HR)
-            def _(r):
-                rr = pl.ds(pl.multiple_of(r * HR, HR), HR)
-                tbuf[p, rr, :] = jnp.dot(xbuf[p, rr, pl.ds(0, FS)], wbuf[...], preferred_element_type=F32)
-
-            cs.wait()
-            cx.wait()
-
-            @pl.loop(0, 2)
-            def _(r):
-                rr = pl.ds(pl.multiple_of(r * HR, HR), HR)
-                m = kk * 4 + p * 2 + r
-                rs_msg(m).wait_recv()
-                cr = pltpu.make_async_copy(rs.at[m], rsv, l_sem.at[2])
-                cr.start()
-                cr.wait()
-                total = tbuf[p, rr, :] + sibv[rr, :] + rsv[...]
-                obuf[rr, :] = (xtv[rr, :].astype(F32) + total).astype(BF16)
-
-            co = pltpu.make_async_copy(obuf, y_ref.at[rows, cols], l_sem.at[2])
-            co.start()
-            co.wait()
-
-    def w2_load(kk):
+
+    def times_w2(s, w, out):
+        @pl.loop(0, KB // HC)
+        def _(r):
+            cc = pl.ds(pl.multiple_of(r * HC, HC), HC)
+            out(cc, jnp.dot(xbuf[s, :, pl.ds(0, FS)], wbuf[w, :, cc], preferred_element_type=F32))
+
+    def w2_load(kk, w):
         @pl.when(kk == 0)
         def _():
-            cp = pltpu.make_async_copy(w2_ref, wbuf, l_sem.at[2])
-            cp.start()
-            cp.wait()
+            pltpu.make_async_copy(w2_ref, wbuf.at[w], w_sem.at[w]).start()
 
         @pl.when(kk > 0)
         def _():
-            cp = pltpu.make_async_copy(w2g.at[col_of(kk)], wbuf, l_sem.at[2])
-            cp.start()
-            cp.wait()
-
-    def own_part(kk):
-        w2_load(kk)
-        finish(kk, col_of(kk), False)
-
-    @pl.loop(0, 9)
-    def _(kk):
-        @pl.when(kk == 1)
-        def _():
-            stage1(w2m)
-
-        @pl.when(kk == 3)
-        def _():
-            stage2(w2m)
-            got(w2m, ("YL", 1), ("YR", 1))
-
-        @pl.when(kk == 5)
-        def _():
-            stage3(w2m)
-            got(w2m, ("YL", 2), ("YR", 2))
-
-        @pl.when(kk == 6)
-        def _():
-            got(w2m, ("BR", 3), ("BL", 3))
-
-        @pl.when(kk == 7)
-        def _():
-            got(w2m, ("YL", 3), ("YR", 3))
-
-        @pl.when(kk < 8)
-        def _():
-            w2_load(kk)
+            pltpu.make_async_copy(w2g.at[col_of(kk)], wbuf.at[w], w_sem.at[w]).start()
+
+    def w2_wait(w):
+        pltpu.make_async_copy(w2_ref, wbuf.at[w], w_sem.at[w]).wait()
+
+    def partner_units(kk, w, first=False):
+        if not first:
             h_load(4, 0).start()
 
-            @pl.loop(0, 4)
-            def _(q):
-                s = q % 2
+        @pl.loop(0, 4)
+        def _(q):
+            s = q % 2
+            n = kk * 4 + q
+            if first:
+                h_tiles(1, lambda t: 4 + q, lambda t: NC - 1)
+                h_load(4 + q, s).start()
+            else:
 
                 @pl.when(q < 3)
                 def _():
                     h_load(5 + q, 1 - s).start()
 
-                h_load(4 + q, s).wait()
-
-                @pl.loop(0, 2)
-                def _(r):
-                    rr = pl.ds(pl.multiple_of(r * HR, HR), HR)
-                    ubuf[s, r] = jnp.dot(xbuf[s, rr, pl.ds(0, FS)], wbuf[...], preferred_element_type=F32)
-
-                dd_msg(kk * 4 + q, s).start()
+            if not first:
 
                 @pl.when(q > 0)
                 def _():
-                    pass_on(kk * 4 + q - 1, 1 - s)
-
-            pass_on(kk * 4 + 3, 1)
-
-            @pl.when(kk == 0)
-            def _():
-                h_tiles(12, lambda n: n % 4, lambda n: 4 + n // 4)
-
+                    pass_start(n - 1, 1 - s)
+
+            if first:
+
+                @pl.when(q == 0)
+                def _():
+                    w2_wait(w)
+
+            h_load(4 + q, s).wait()
+
+            def out(cc, val):
+                ubuf[s, 0, :, cc] = val[:HR]
+                ubuf[s, 1, :, cc] = val[HR:]
+
+            times_w2(s, w, out)
+            dd_msg(n, s).start()
+
+            if first:
+                pass_start(n, s)
+                pass_sum(n, s)
+                pass_send(n)
+            else:
+
+                @pl.when(q > 0)
+                def _():
+                    pass_sum(n - 1, 1 - s)
+                    pass_send(n - 1)
+
+        if not first:
+            n = kk * 4 + 3
             h_load(2, 0).start()
             h_load(3, 1).start()
-
-            @pl.loop(0, 2)
-            def _(p):
-                h_load(2 + p, p).wait()
-
-                @pl.loop(0, PR // HR)
-                def _(r):
-                    rr = pl.ds(pl.multiple_of(r * HR, HR), HR)
-                    tbuf[p, rr, :] = jnp.dot(xbuf[p, rr, pl.ds(0, FS)], wbuf[...], preferred_element_type=F32)
-
-                sp_msg(kk * 2 + p, p).start()
-
-            for p in range(2):
-                sp_msg(kk * 2 + p, p).wait_send()
-
-        @pl.when(kk > 0)
-        def _():
-            own_part(kk - 1)
+            pass_start(n, 1)
+            pass_sum(n, 1)
+            pass_send(n)
+
+    def sibling_units(kk, w):
+        @pl.loop(0, 2)
+        def _(p):
+            h_load(2 + p, p).wait()
+
+            @pl.when(kk > 0)
+            def _():
+                sp_msg(kk * 2 + p - 2, p).wait_send()
+
+            def out(cc, val):
+                tbuf[p, :, cc] = val
+
+            times_w2(p, w, out)
+            sp_msg(kk * 2 + p, p).start()
+
+    def finish(kk, w):
+        for p in range(2):
+            h_load(p, p).start()
+        cols = pl.ds(pl.multiple_of(col_of(kk) * KB, KB), KB)
+
+        @pl.loop(0, 2)
+        def _(p):
+            rows = pl.ds(pl.multiple_of(p * PR, PR), PR)
+            n = kk * 2 + p
+            cx = pltpu.make_async_copy(x_ref.at[rows, cols], xtv, l_sem.at[2])
+            cx.start()
+            sp_msg(n, p).wait_recv()
+            cs = pltpu.make_async_copy(sibp.at[n], sibv, l_sem.at[3])
+            cs.start()
+            h_load(p, p).wait()
+
+            def out(cc, val):
+                ybuf[:, cc] = val
+
+            times_w2(p, w, out)
+            cs.wait()
+            cx.wait()
+            for r in range(2):
+                rs_msg(kk * 4 + p * 2 + r).wait_recv()
+                pltpu.make_async_copy(rs.at[kk * 4 + p * 2 + r], rsv.at[r], l_sem.at[2 + r]).start()
+
+            co = pltpu.make_async_copy(obuf, y_ref.at[rows, cols], o_sem)
+            for r in range(2):
+                rr = pl.ds(r * HR, HR)
+                pltpu.make_async_copy(rs.at[kk * 4 + p * 2 + r], rsv.at[r], l_sem.at[2 + r]).wait()
+                if r == 0:
+
+                    @pl.when(n > 0)
+                    def _():
+                        co.wait()
+
+                total = ybuf[rr, :] + sibv[rr, :] + rsv[r]
+                obuf[rr, :] = (xtv[rr, :].astype(F32) + total).astype(BF16)
+            co.start()
+
+    w2_load(0, 0)
+    partner_units(0, 0, True)
+    h_tiles(2, lambda n: 2 + n, lambda n: 4)
+
+    @pl.loop(1, 11)
+    def _(kk):
+        w = kk % 4
+
+        @pl.when(kk == 1)
+        def _():
+            got(w2m, ("R", 0), ("L", 0), ("R", 1), ("L", 1))
+            send(w2m, ("R", 2), ("L", 2), ("YL", 1), ("YR", 1))
+
+        @pl.when(kk == 2)
+        def _():
+            got(w2m, "Y0")
+            send(w2m, ("BR", 1), ("BL", 1))
+
+        @pl.when(kk == 3)
+        def _():
+            stage2(w2m)
+
+        @pl.when(kk == 4)
+        def _():
+            got(w2m, ("YL", 1), ("YR", 1))
+
+        @pl.when(kk == 5)
+        def _():
+            stage3(w2m)
+
+        @pl.when(kk == 6)
+        def _():
+            got(w2m, ("YL", 2), ("YR", 2))
+
+        @pl.when(kk == 7)
+        def _():
+            got(w2m, ("YL", 3), ("YR", 3), ("BR", 3), ("BL", 3))
+
+        @pl.when(kk < 8)
+        def _():
+            w2_load(kk, w)
+            w2_wait(w)
+            partner_units(kk, w)
+
+        @pl.when(kk == 2)
+        def _():
+            h_load(2, 0).wait()
+            h_load(3, 1).wait()
+            h_tiles(10, lambda n: n % 4, lambda n: 6 - n // 4)
+            h_load(2, 0).start()
+            h_load(3, 1).start()
+            sibling_units(0, 0)
+            h_load(2, 0).start()
+            h_load(3, 1).start()
+
+        @pl.when(kk == 8)
+        def _():
+            h_load(2, 0).start()
+            h_load(3, 1).start()
+
+        @pl.when((kk > 1) & (kk < 9))
+        def _():
+            sibling_units(kk - 1, (kk + 3) % 4)
+
+        @pl.when(kk == 1)
+        def _():
+            h_load(2, 0).wait()
+            h_load(3, 1).wait()
+
+        @pl.when(kk > 2)
+        def _():
+            finish(kk - 3, (kk + 1) % 4)
+
+    pltpu.make_async_copy(obuf, y_ref.at[pl.ds(0, PR), pl.ds(0, KB)], o_sem).wait()
+    for p in range(2):
+        sp_msg(14 + p, p).wait_send()
 
     for m in (*w1m, w2m):
         for cp, sent, _ in m.values():
@@ -461,19 +559,20 @@
             pltpu.VMEM((NC, D, CW), BF16),
             pltpu.VMEM((2, PR, D), BF16),
             pltpu.VMEM((2, PR, CW), BF16),
-            pltpu.VMEM((FS, KB), BF16),
+            pltpu.VMEM((4, FS, KB), BF16),
             pltpu.VMEM((2, 2, HR, KB), F32),
             pltpu.VMEM((HR, KB), F32),
             pltpu.VMEM((HR, KB), F32),
             pltpu.VMEM((2, PR, KB), F32),
             pltpu.VMEM((PR, KB), F32),
-            pltpu.VMEM((HR, KB), F32),
+            pltpu.VMEM((PR, KB), F32),
+            pltpu.VMEM((2, HR, KB), F32),
             pltpu.VMEM((PR, KB), BF16),
             pltpu.VMEM((PR, KB), BF16),
             pltpu.SemaphoreType.DMA((NC, 19)),
             pltpu.SemaphoreType.DMA((NC, 19)),
-            pltpu.SemaphoreType.DMA((19,)),
-            pltpu.SemaphoreType.DMA((19,)),
+            pltpu.SemaphoreType.DMA((21,)),
+            pltpu.SemaphoreType.DMA((21,)),
             pltpu.SemaphoreType.DMA((12,)),
             pltpu.SemaphoreType.DMA((12,)),
             pltpu.SemaphoreType.DMA((2,)),
@@ -484,6 +583,8 @@
             pltpu.SemaphoreType.DMA((16,)),
             pltpu.SemaphoreType.DMA((4,)),
             pltpu.SemaphoreType.DMA((NC,)),
+            pltpu.SemaphoreType.DMA((4,)),
+            pltpu.SemaphoreType.DMA,
         ],
         compiler_params=pltpu.CompilerParams(
             collective_id=0, has_side_effects=True, vmem_limit_bytes=67000000

time: 759 us -> 703 us (0.926)
  the two profiles are of different devices: /device:TPU:18 before, /device:TPU:0 now
where the time goes in v3:
time: 703 us; the launch traced here: 701 us
  Pallas kernels  693 us (99%)
  local copies, waits for them, and re-layouts  7.89 us (1%)
    pallas_call x1, Pallas kernels, _block(): pl.pallas_call(_kernel, name='mlp', out_shape=[jax.ShapeDtypeStruct((ROWS...  693 us

profile of v3, /device:TPU:0, one launch (start us, length us, event | category | flops | bytes accessed | tf_op | source)
XLA Modules:
  0.0 700.8 jit_solution(9241780215808440031)
XLA Ops:
  0.0 692.9 %mlp.1 = (bf16[1024,4096]{1,0:T(8,128)(2,1)}, bf16[4096,4096]{1,0:T(8,128)(2,1)}, bf16[4096,3584]{1,0:T(8,128)(2,1)}, bf16[8,3584,512]{2,1,0:T(8,128)(2,1)}, f32...) custom-call(bf16[1024,4096]{1,0:T(8,128)(2,1)} %x_ref.1, ...), custom_call_target="tpu_custom_call" | custom-call | tf_op jit(solution)/shard_map/mlp/pallas_call | solution.py:543
  692.9 7.9 %copy.6 = bf16[1024,4096]{1,0:T(8,128)(2,1)} copy(bf16[1024,4096]{1,0:T(8,128)(2,1)} %get-tuple-element.6) | data formatting | bytes 16777216

commit v4 on v3

--- a/solution.py
+++ b/solution.py
@@ -58,22 +58,27 @@
         def blk(dz, dy):
             return (z + dz) * 2 + (1 - yq if dy else yq)
 
-        def add(key, dev, dz, dy, lo, cnt, sent, got, first=False):
+        def add(key, dev, dz, dy, lo, cnt, sent, got, first=False, part=None):
             i = len(m)
-            dst = reg(blk(dz, dy), lo, cnt)
-            m[key] = (remote(own(lo, cnt) if first else dst, dst, send(i), recv(i), dev), sent, got)
+            dst = reg(blk(dz, dy), lo, cnt, part)
+            m[key] = (remote(own(lo, cnt, part) if first else dst, dst, send(i), recv(i), dev), sent, got)
 
         always = None
-        add("Y0", to_yy, 0, 0, 0, n, always, always, True)
+        if lead:
+            add("Y0", to_yy, 0, 0, 0, n, always, always, True, 0)
+            add("Y1", to_yy, 0, 0, 0, n, always, always, True, 1)
+            add(("R", 0), to_zp, 0, 0, 0, lead, z <= 2, z >= 1, True)
+            add(("L", 0), to_zm, 0, 0, 0, lead, z >= 1, z <= 2, True)
+        else:
+            add("Y0", to_yy, 0, 0, 0, n, always, always, True)
         for d in (1, 2, 3):
             right = (z <= 2) & (z >= d - 1)
             left = (z >= 1) & (z <= 4 - d)
             skip = lead if d == 1 else 0
-            if skip:
-                add(("R", 0), to_zp, 0, 0, 0, skip, right, z >= 1, True)
-                add(("L", 0), to_zm, 0, 0, 0, skip, left, z <= 2, True)
-            add(("R", d), to_zp, 1 - d, 0, skip, n - skip, right, z >= d, d == 1)
-            add(("L", d), to_zm, d - 1, 0, skip, n - skip, left, z <= 3 - d, d == 1)
+            for part in (0, 1) if lead and d < 3 else (None,):
+                k = (d,) if part is None else (d, part)
+                add(("R", *k), to_zp, 1 - d, 0, skip, n - skip, right, z >= d, d == 1, part)
+                add(("L", *k), to_zm, d - 1, 0, skip, n - skip, left, z <= 3 - d, d == 1, part)
             add(("YL", d), to_yy, -d, 0, 0, cut, z >= d, z >= d)
             add(("YR", d), to_yy, d, 0, 0, cut, z <= 3 - d, z <= 3 - d)
             add(("BR", d), to_zp, 1 - d, 1, cut, n - cut, right, z >= d)
@@ -121,10 +126,10 @@
         got(m, ("BR", 3), ("BL", 3))
 
     def w1_messages(j):
-        def reg(s, lo, n):
+        def reg(s, lo, n, part):
             return w1v.at[j, pl.ds(pl.multiple_of(s * KB + lo, 16), n), :]
 
-        def own(lo, n):
+        def own(lo, n, part):
             return w1_ref.at[pl.ds(lo, n), pl.ds(j * CW, CW)]
 
         return messages(reg, own, lambda i: w1_send.at[j, i], lambda i: w1_recv.at[j, i], KB, CUT1, 0)
@@ -152,9 +157,12 @@
         stage4(w1m[j])
         loc[j].wait()
 
+    def half(part):
+        return slice(None) if part is None else pl.ds(part * HC, HC)
+
     w2m = messages(
-        lambda s, lo, n: w2g.at[s, pl.ds(lo, n), :],
-        lambda lo, n: w2_ref.at[pl.ds(lo, n), :],
+        lambda s, lo, n, part: w2g.at[s, pl.ds(lo, n), half(part)],
+        lambda lo, n, part: w2_ref.at[pl.ds(lo, n), half(part)],
         lambda i: w2_send.at[i], lambda i: w2_recv.at[i], FS, CUT2, LEAD2,
     )
 
@@ -251,7 +259,7 @@
         if t == NC:
             send(w2m, ("R", 0), ("L", 0))
         if t == NC + 1:
-            stage0(w2m)
+            send(w2m, ("R", 1, 0), ("L", 1, 0), "Y0", ("R", 1, 1), ("L", 1, 1), "Y1")
         if t in (1, 2):
             forward_x(t - 1)
         if t < 3:
@@ -284,12 +292,17 @@
         return sum(jnp.where(kk == k, v, 0) for k, v in enumerate(values) if v)
 
     def col_of(kk):
-        i = pick(kk, (0, 1, 0, 2, 1, 3, 2, 3))
-        dy = pick(kk, (0, 0, 1, 0, 1, 0, 1, 1))
+        i = pick(kk, (0, 1, 0, 1, 2, 2, 3, 3))
+        dy = pick(kk, (0, 0, 1, 1, 0, 1, 0, 1))
         e = jnp.where(z < 2, z, 3 - z)
         v = jnp.where(i <= e, i - 1, i)
         v = jnp.where(z < 2, v, 3 - v)
+        v = jnp.where(z == 2, pick(i, (0, 1, 3, 0)), v)
         return jnp.where(i == 0, z, v) * 2 + lax.rem(yq + dy, 2)
+
+    def source(kk, h):
+        mixed = (kk == 1) | (kk == 2)
+        return col_of(jnp.where(mixed, 1 + h, kk)), pl.multiple_of(jnp.where(mixed, kk - 1, h) * HC, HC)
 
     def dd_msg(n, s):
         return remote(ubuf.at[s, 1 - c], d2d.at[n], dd_send.at[s], dd_recv.at[n], sib)
@@ -333,7 +346,10 @@
 
         @pl.when(kk > 0)
         def _():
-            pltpu.make_async_copy(w2g.at[col_of(kk)], wbuf.at[w], w_sem.at[w]).start()
+            for h in range(2):
+                shard, off = source(kk, h)
+                src = w2g.at[shard, :, pl.ds(off, HC)]
+                pltpu.make_async_copy(src, wbuf.at[w, :, pl.ds(h * HC, HC)], w_sem.at[w]).start()
 
     def w2_wait(w):
         pltpu.make_async_copy(w2_ref, wbuf.at[w], w_sem.at[w]).wait()
@@ -413,14 +429,18 @@
     def finish(kk, w):
         for p in range(2):
             h_load(p, p).start()
-        cols = pl.ds(pl.multiple_of(col_of(kk) * KB, KB), KB)
+        cols = []
+        for h in range(2):
+            shard, off = source(kk, h)
+            cols.append(pl.ds(pl.multiple_of(shard * KB + off, HC), HC))
 
         @pl.loop(0, 2)
         def _(p):
             rows = pl.ds(pl.multiple_of(p * PR, PR), PR)
             n = kk * 2 + p
-            cx = pltpu.make_async_copy(x_ref.at[rows, cols], xtv, l_sem.at[2])
-            cx.start()
+            cx = [pltpu.make_async_copy(x_ref.at[rows, cols[h]], xtv.at[:, half(h)], l_sem.at[2]) for h in range(2)]
+            for cp in cx:
+                cp.start()
             sp_msg(n, p).wait_recv()
             cs = pltpu.make_async_copy(sibp.at[n], sibv, l_sem.at[3])
             cs.start()
@@ -431,12 +451,12 @@
 
             times_w2(p, w, out)
             cs.wait()
-            cx.wait()
+            pltpu.make_async_copy(x_ref.at[rows, pl.ds(0, KB)], xtv, l_sem.at[2]).wait()
             for r in range(2):
                 rs_msg(kk * 4 + p * 2 + r).wait_recv()
                 pltpu.make_async_copy(rs.at[kk * 4 + p * 2 + r], rsv.at[r], l_sem.at[2 + r]).start()
 
-            co = pltpu.make_async_copy(obuf, y_ref.at[rows, cols], o_sem)
+            co = [pltpu.make_async_copy(obuf.at[:, half(h)], y_ref.at[rows, cols[h]], o_sem) for h in range(2)]
             for r in range(2):
                 rr = pl.ds(r * HR, HR)
                 pltpu.make_async_copy(rs.at[kk * 4 + p * 2 + r], rsv.at[r], l_sem.at[2 + r]).wait()
@@ -444,48 +464,50 @@
 
                     @pl.when(n > 0)
                     def _():
-                        co.wait()
+                        pltpu.make_async_copy(obuf, y_ref.at[rows, pl.ds(0, KB)], o_sem).wait()
 
                 total = ybuf[rr, :] + sibv[rr, :] + rsv[r]
                 obuf[rr, :] = (xtv[rr, :].astype(F32) + total).astype(BF16)
-            co.start()
+            for cp in co:
+                cp.start()
 
     w2_load(0, 0)
     partner_units(0, 0, True)
-    h_tiles(2, lambda n: 2 + n, lambda n: 4)
-
-    @pl.loop(1, 11)
+
+    inner = (z == 1) | (z == 2)
+
+    @pl.loop(1, 10)
     def _(kk):
         w = kk % 4
 
         @pl.when(kk == 1)
         def _():
-            got(w2m, ("R", 0), ("L", 0), ("R", 1), ("L", 1))
-            send(w2m, ("R", 2), ("L", 2), ("YL", 1), ("YR", 1))
+            got(w2m, ("R", 0), ("L", 0), ("R", 1, 0), ("L", 1, 0), "Y0")
+            send(w2m, ("R", 2, 0), ("L", 2, 0))
 
         @pl.when(kk == 2)
         def _():
-            got(w2m, "Y0")
-            send(w2m, ("BR", 1), ("BL", 1))
+            got(w2m, ("R", 1, 1), ("L", 1, 1), "Y1")
+            send(w2m, ("YL", 1), ("YR", 1), ("BR", 1), ("BL", 1), ("R", 2, 1), ("L", 2, 1))
 
         @pl.when(kk == 3)
         def _():
-            stage2(w2m)
-
-        @pl.when(kk == 4)
-        def _():
-            got(w2m, ("YL", 1), ("YR", 1))
+            pl.when(z == 0)(w2m["YR", 1][0].wait_recv)
+            pl.when(z > 0)(w2m["YL", 1][0].wait_recv)
+            got(w2m, ("BR", 1), ("BL", 1))
 
         @pl.when(kk == 5)
         def _():
-            stage3(w2m)
-
-        @pl.when(kk == 6)
-        def _():
-            got(w2m, ("YL", 2), ("YR", 2))
+            pl.when(z == 0)(w2m["YR", 2][0].wait_recv)
+            pl.when(z == 3)(w2m["YL", 2][0].wait_recv)
+            pl.when(inner)(w2m["YR", 1][0].wait_recv)
+            got(w2m, ("BR", 2), ("BL", 2))
 
         @pl.when(kk == 7)
         def _():
+            finish(4, 0)
+            pl.when(z == 1)(w2m["YR", 2][0].wait_recv)
+            pl.when(z == 2)(w2m["YL", 2][0].wait_recv)
             got(w2m, ("YL", 3), ("YR", 3), ("BR", 3), ("BL", 3))
 
         @pl.when(kk < 8)
@@ -494,11 +516,21 @@
             w2_wait(w)
             partner_units(kk, w)
 
+        @pl.when(kk == 3)
+        def _():
+            got(w2m, ("R", 2, 0), ("L", 2, 0), ("R", 2, 1), ("L", 2, 1))
+            send(w2m, ("BR", 2), ("BL", 2), ("R", 3), ("L", 3), ("YL", 2), ("YR", 2))
+
+        @pl.when(kk == 5)
+        def _():
+            got(w2m, ("R", 3), ("L", 3))
+            send(w2m, ("BR", 3), ("BL", 3), ("YL", 3), ("YR", 3))
+
         @pl.when(kk == 2)
         def _():
             h_load(2, 0).wait()
             h_load(3, 1).wait()
-            h_tiles(10, lambda n: n % 4, lambda n: 6 - n // 4)
+            h_tiles(12, lambda n: n % 4, lambda n: 4 + n // 4)
             h_load(2, 0).start()
             h_load(3, 1).start()
             sibling_units(0, 0)
@@ -521,7 +553,8 @@
 
         @pl.when(kk > 2)
         def _():
-            finish(kk - 3, (kk + 1) % 4)
+            n = jnp.where(kk < 7, kk - 3, kk - 2)
+            finish(n, n % 4)
 
     pltpu.make_async_copy(obuf, y_ref.at[pl.ds(0, PR), pl.ds(0, KB)], o_sem).wait()
     for p in range(2):
@@ -571,8 +604,8 @@
             pltpu.VMEM((PR, KB), BF16),
             pltpu.SemaphoreType.DMA((NC, 19)),
             pltpu.SemaphoreType.DMA((NC, 19)),
-            pltpu.SemaphoreType.DMA((21,)),
-            pltpu.SemaphoreType.DMA((21,)),
+            pltpu.SemaphoreType.DMA((26,)),
+            pltpu.SemaphoreType.DMA((26,)),
             pltpu.SemaphoreType.DMA((12,)),
             pltpu.SemaphoreType.DMA((12,)),
             pltpu.SemaphoreType.DMA((2,)),

time: 703 us -> 700 us (level)
  no operation moved by 1% of the time
where the time goes in v4:
time: 700 us; the launch traced here: 699 us
  Pallas kernels  691 us (99%)
  local copies, waits for them, and re-layouts  7.89 us (1%)
    pallas_call x1, Pallas kernels, _block(): pl.pallas_call(_kernel, name='mlp', out_shape=[jax.ShapeDtypeStruct((ROWS...  691 us

profile of v4, /device:TPU:0, one launch (start us, length us, event | category | flops | bytes accessed | tf_op | source)
XLA Modules:
  0.0 698.8 jit_solution(5784744368425422662)
XLA Ops:
  0.0 690.9 %mlp.1 = (bf16[1024,4096]{1,0:T(8,128)(2,1)}, bf16[4096,4096]{1,0:T(8,128)(2,1)}, bf16[4096,3584]{1,0:T(8,128)(2,1)}, bf16[8,3584,512]{2,1,0:T(8,128)(2,1)}, f32...) custom-call(bf16[1024,4096]{1,0:T(8,128)(2,1)} %x_ref.1, ...), custom_call_target="tpu_custom_call" | custom-call | tf_op jit(solution)/shard_map/mlp/pallas_call | solution.py:576
  690.9 7.9 %copy.6 = bf16[1024,4096]{1,0:T(8,128)(2,1)} copy(bf16[1024,4096]{1,0:T(8,128)(2,1)} %get-tuple-element.6) | data formatting | bytes 16777216
